TPU v7x, 32 devices: a whole 2x2x4 slice. The times are simulated.
32 devices in a mesh: dp: 8 (over z, y), expert: 2 (over core), tensor: 2 (over x).
Axes of the slice: x: 2, y: 2, z: 4, core: 2. Of those that a mesh axis runs over, the one named last changes fastest.
Arguments:
- dense_act: bfloat16 [2, 32, 512, 3584], P(None, 'dp', 'expert', 'tensor'), may hold values from -6 to 6
- dense_cot: bfloat16 [2, 32, 512, 3584], P(None, 'dp', ('expert', 'tensor')), may hold values from -6 to 6
- dense_proj_in: bfloat16 [2, 3584, 128], P(None, 'tensor'), may hold values from -0.09375 to 0.09375
- dense_proj_out: bfloat16 [2, 3584, 128], replicated, may hold values from -0.09375 to 0.09375
- expert_act: bfloat16 [32, 8, 64, 2560], P('dp', 'expert', None, 'tensor'), may hold values from -6 to 6
- expert_cot: bfloat16 [32, 8, 64, 3584], P('dp', 'expert', 'tensor'), may hold values from -6 to 6
- expert_proj_in: bfloat16 [2560, 128], P('tensor'), may hold values from -0.125 to 0.125
- expert_proj_out: bfloat16 [3584, 128], replicated, may hold values from -0.09375 to 0.09375
- dense_valid: float32 [2, 128, 128], replicated, may hold values from -0.0012207031 to 0.0012207031
- expert_valid: float32 [8, 128, 128], P('expert'), may hold values from -0.0012207031 to 0.0012207031
- domain_ids: int32 [32], P('dp'), may hold values from 0 to 63
- prior_mix: float32 [64], replicated, may hold values from 0.002 to 0.05
Outputs:
- log_mixture_weights: float32 [64], P('dp')
All inputs are finite; a program needn't handle non-finite values.
Results may differ from a plain program's by a relative error of at most 0.0003.
Values sent between devices are 32-bit elements; how exact they have to be, the bound alone decides.
A program may use at most 128 MiB of HBM per device.

v0:
```python
import jax
import jax.numpy as jnp
from jax import lax
from jax.sharding import PartitionSpec as P


def per_device(
    dense_act,
    dense_cot,
    dense_proj_in,
    dense_proj_out,
    expert_act,
    expert_cot,
    expert_proj_in,
    expert_proj_out,
    dense_valid,
    expert_valid,
    domain_ids,
    prior_mix,
):
    block = dense_act
    dense_update_vector = lax.psum_scatter(
        jnp.einsum("lmtd,ldr->tlmr", block, dense_proj_in, preferred_element_type=jnp.float32),
        "tensor",
        scatter_dimension=0,
        tiled=True,
    )
    dense_weight_matrix = jnp.einsum(
        "lmtd,ldr->tlmr", dense_cot, dense_proj_out, preferred_element_type=jnp.float32
    )
    dense_portion = jnp.einsum(
        "fquy,fquh->quyh", dense_update_vector, dense_weight_matrix, precision=lax.Precision.HIGHEST
    )
    block = expert_act
    expert_u = lax.psum_scatter(
        jnp.einsum("mecf,fr->cmer", block, expert_proj_in, preferred_element_type=jnp.float32),
        "tensor",
        scatter_dimension=0,
        tiled=True,
    )
    expert_weight_matrix = jnp.einsum(
        "mecd,dr->cmer", expert_cot, expert_proj_out, preferred_element_type=jnp.float32
    )
    expert_part = jnp.einsum(
        "cmer,cmes->mers", expert_u, expert_weight_matrix, precision=lax.Precision.HIGHEST
    )
    dense_full = lax.psum(dense_portion, ("expert", "tensor"))
    dense_score = jnp.sum(dense_full * dense_valid[:, None], axis=(0, 2, 3))
    expert_full = lax.psum(expert_part, "tensor")
    expert_local = jnp.sum(expert_full * expert_valid[None], axis=(1, 2, 3))
    score = dense_score + lax.psum(expert_local, "expert")
    domains = prior_mix.shape[0]
    onehot = (domain_ids[:, None] == jnp.arange(domains, dtype=jnp.int32)[None, :]).astype(
        jnp.float32
    )
    domain_part = jnp.dot(score, onehot, precision=lax.Precision.HIGHEST)
    share_tally_count = domains // lax.axis_size("dp")
    first_domain = lax.axis_index("dp") * share_tally_count
    previous_domain_share = lax.dynamic_slice_in_dim(prior_mix, first_domain, share_tally_count, 0)
    domain_total = lax.psum(domain_part, "dp")
    spread = jnp.sqrt(jnp.mean(domain_total * domain_total) + 1e-06)
    z_value = domain_total / spread
    mass = jnp.sum(prior_mix * jnp.exp(0.5 * z_value))
    z_share = lax.dynamic_slice_in_dim(z_value, first_domain, share_tally_count, 0)
    return jnp.log(previous_domain_share) + 0.5 * z_share - jnp.log(mass)


def solution(mesh):
    placed = (
        P(None, "dp", "expert", "tensor"),
        P(None, "dp", ("expert", "tensor"), None),
        P(None, "tensor", None),
        P(),
        P("dp", "expert", None, "tensor"),
        P("dp", "expert", "tensor", None),
        P("tensor", None),
        P(),
        P(),
        P("expert", None, None),
        P("dp"),
        P(),
    )
    return jax.shard_map(per_device, mesh=mesh, in_specs=placed, out_specs=P("dp"), check_vma=False)
```

profile of v0, /device:TPU:0, one launch (start us, length us, event | category | flops | bytes accessed | tf_op | source)
XLA Modules:
  0.0 206.4 jit_solution(693878961875852554)
XLA Ops:
  6.5 0.0 copy-start
  6.5 0.0 copy-start.3
  6.5 0.0 all-reduce.9.cloned.1.call-start
  6.5 1.7 copy-done
  8.3 1.8 convolution_bitcast_fusion.1
  10.1 1.1 copy.18
  11.2 0.0 all-reduce.9.cloned.1.call-update
  11.3 0.0 reduce-scatter.4.cloned.1.call-start
  11.3 0.0 copy-done.3
  11.3 5.6 %convolution_bitcast_fusion = f32[256,2,4,128]{0,3,2,1:T(8,128)S(1)} fusion(bf16[2,4,256,1792]{3,2,1,0:T(8,128)(2,1)} %param.12, bf16[2,1792,128]{2,1,0:T(8,128)(2,1)S(1)} %copy-done.3), kind=kOutput, calls=%fused_computation.2 | convolution fusion | flops 939524096 | bytes 9306112 | tf_op jit(solution)/shard_map/lmtd,ldr->tlmr/dot_general | solution.py:23
  16.9 26.2 %copy.29 = f32[256,2,4,128]{2,3,1,0:T(8,128)} copy(f32[256,2,4,128]{0,3,2,1:T(8,128)S(1)} %convolution_bitcast_fusion) | data formatting | bytes 2097152
  43.2 0.0 copy-start.9
  43.2 0.0 copy-start.7
  43.2 29.4 %reshape.9 = f32[256,1024]{1,0:T(8,128)} reshape(f32[256,2,128,4]{3,2,1,0:T(8,128)} %bitcast.46) | data formatting | bytes 2097152
  72.5 0.0 reduce-scatter.4.cloned.1.call-update
  72.6 0.0 all-reduce.7.cloned.1.call-start
  72.6 0.0 copy-done.9
  72.6 0.6 dynamic-slice
  73.9 0.0 copy-done.7
  73.9 0.0 copy-start.2
  73.9 3.3 %fusion.6 = f32[128,4,4,32]{0,3,2,1:T(8,128)S(1)} fusion(bf16[4,4,32,3584]{3,2,1,0:T(8,128)(2,1)} %param.17, bf16[3584,128]{1,0:T(8,128)(2,1)S(1)} %copy-done.7), kind=kOutput, calls=%fused_computation.8 | convolution fusion | flops 469762048 | bytes 4849664 | tf_op jit(solution)/shard_map/mecd,dr->cmer/dot_general | solution.py:41
  77.2 0.0 all-reduce.9.cloned.1.call-done
  77.2 1.0 constant_dynamic-slice_fusion
  78.2 2.8 %fusion.9 = f32[4,4,128,128]{3,2,1,0:T(8,128)} fusion(f32[128,4,4,32]{0,3,2,1:T(8,128)S(1)} %fusion.6, f32[32,4,4,128]{3,2,1,0:T(4,128)S(1)} %constant_dynamic-slice_fusion), kind=kOutput, calls=%fused_computation.12 | convolution fusion | flops 100663296 | bytes 1572864 | tf_op jit(solution)/shard_map/cmer,cmes->mers/dot_general | solution.py:44
  81.0 0.0 all-reduce.7.cloned.1.call-update
  81.0 0.2 all-reduce.5.cloned.1.call-start
  81.3 0.0 copy-done.2
  81.3 5.6 %fusion.2 = f32[128,2,4,128]{0,3,2,1:T(8,128)S(1)} fusion(bf16[2,4,128,3584]{3,2,1,0:T(8,128)(2,1)} %param.13, bf16[2,3584,128]{2,1,0:T(8,128)(2,1)S(1)} %copy-done.2), kind=kOutput, calls=%fused_computation.3 | convolution fusion | flops 939524096 | bytes 9699328 | tf_op jit(solution)/shard_map/lmtd,ldr->tlmr/dot_general | solution.py:28
  86.9 8.9 %reduce-scatter.4.cloned.1.call-done = f32[128,1024]{1,0:T(8,128)} async-done(((f32[256,1024]{1,0:T(8,128)}), f32[128,1024]{1,0:T(8,128)}) %reduce-scatter.4.cloned.1.call-update) | async-done | bytes 524304
  95.8 19.5 %reshape.10 = f32[128,2,128,4]{3,2,1,0:T(8,128)} reshape(f32[128,1024]{1,0:T(8,128)} %reduce-scatter.4.cloned.1.call-done) | data formatting | bytes 1048576
  115.3 0.0 copy-start.4
  115.3 0.0 copy-start.5
  115.3 0.0 copy-start.1
  115.3 13.2 %copy.16 = f32[128,2,4,128]{0,3,2,1:T(8,128)} copy(f32[128,2,4,128]{2,3,1,0:T(8,128)} %bitcast.47) | data formatting | bytes 1048576 | tf_op jit(solution)/shard_map/reduce_scatter | solution.py:22
  128.5 0.0 copy-start.8
  128.5 0.0 copy-start.6
  128.5 3.1 %fusion.12 = f32[2,4,128,128]{3,2,1,0:T(8,128)} fusion(f32[128,2,4,128]{0,3,2,1:T(8,128)} %copy.16, f32[128,2,4,128]{0,3,2,1:T(8,128)S(1)} %fusion.2), kind=kOutput, calls=%fused_computation.22 | convolution fusion | flops 201326592 | bytes 1572864 | tf_op jit(solution)/shard_map/fquy,fquh->quyh/dot_general | solution.py:31
  131.6 0.0 all-reduce.5.cloned.1.call-update
  131.6 6.7 %all-reduce.7.cloned.1.call-done = f32[4,4,128,128]{3,2,1,0:T(8,128)} async-done(((f32[4,4,128,128]{3,2,1,0:T(8,128)}), f32[4,4,128,128]{3,2,1,0:T(8,128)}) %all-reduce.7.cloned.1.call-update) | async-done | bytes 1048592 | tf_op jit(solution)/shard_map/psum | solution.py:49
  138.3 0.0 copy-done.4
  138.3 1.4 multiply_reduce_fusion
  139.7 2.4 %psum.30 = f32[4]{0:T(128)S(1)} all-reduce(f32[4]{0:T(128)S(1)} %multiply_reduce_fusion), channel_id=1, replica_groups=mesh['dp'=8,'expert'=2,'tensor'=2] {'expert'}, use_global_device_ids=true, to_apply=%region_6.0 | all-reduce | flops 4 | bytes 32 | tf_op jit(solution)/shard_map/psum | solution.py:51
  142.1 31.8 %all-reduce.5.cloned.1.call-done = f32[2,4,128,128]{3,2,1,0:T(8,128)} async-done(((f32[2,4,128,128]{3,2,1,0:T(8,128)}), f32[2,4,128,128]{3,2,1,0:T(8,128)}) %all-reduce.5.cloned.1.call-update) | async-done | bytes 524304 | tf_op jit(solution)/shard_map/psum | solution.py:47
  173.9 0.0 copy-done.5
  173.9 1.2 multiply_reduce_fusion.1
  175.1 0.0 copy-done.8
  175.1 0.2 convolution_bitcast_fusion.2
  175.3 21.3 %psum.31 = f32[64]{0:T(128)S(1)} all-reduce(f32[64]{0:T(128)S(1)} %convolution_bitcast_fusion.2), channel_id=1, replica_groups=mesh['dp'=8,'expert'=2,'tensor'=2] {'dp'}, use_global_device_ids=true, to_apply=%region_7.0 | all-reduce | flops 64 | bytes 512 | tf_op jit(solution)/shard_map/psum | solution.py:60
  196.7 0.6 multiply_reduce_fusion.3
  198.0 0.0 copy-done.6
  198.0 0.6 multiply_reduce_fusion.2
  199.3 0.6 add_subtract_fusion
  199.9 0.0 copy-done.1
Async XLA Ops:
  6.5 1.7 copy-start
  6.5 4.8 %copy-start.3 = (bf16[2,1792,128]{2,1,0:T(8,128)(2,1)S(1)}, bf16[2,1792,128]{2,1,0:T(8,128)(2,1)}, u32[]{:S(2)}) copy-start(bf16[2,1792,128]{2,1,0:T(8,128)(2,1)} %param.14) | copy-start | bytes 2752516
  6.5 70.6 %all-reduce.9.cloned.1.call-start = ((), (), s32[]{:S(2)}) async-start(), calls=%async_computation.4 | async-start | bytes 1048576
  11.3 84.6 %reduce-scatter.4.cloned.1.call-start = ((), (), s32[]{:S(2)}) async-start(), calls=%async_computation.3 | async-start | bytes 1572864
  43.2 29.4 %copy-start.9 = (u32[32]{0:T(128)S(1)}, u32[32]{0:T(128)}, u32[]{:S(2)}) copy-start(u32[32]{0:T(128)} %constant.29) | copy-start | bytes 388
  43.2 30.7 %copy-start.7 = (bf16[3584,128]{1,0:T(8,128)(2,1)S(1)}, bf16[3584,128]{1,0:T(8,128)(2,1)}, u32[]{:S(2)}) copy-start(bf16[3584,128]{1,0:T(8,128)(2,1)} %param.19) | copy-start | bytes 2752516
  72.6 65.7 %all-reduce.7.cloned.1.call-start = ((), (), s32[]{:S(2)}) async-start(), calls=%async_computation.2 | async-start | bytes 2097152 | tf_op jit(solution)/shard_map/psum | solution.py:49
  73.9 7.4 %copy-start.2 = (bf16[2,3584,128]{2,1,0:T(8,128)(2,1)S(1)}, bf16[2,3584,128]{2,1,0:T(8,128)(2,1)}, u32[]{:S(2)}) copy-start(bf16[2,3584,128]{2,1,0:T(8,128)(2,1)} %param.15) | copy-start | bytes 5505028
  81.0 92.9 %all-reduce.5.cloned.1.call-start = ((), (), s32[]{:S(2)}) async-start(), calls=%async_computation.1 | async-start | bytes 1048576 | tf_op jit(solution)/shard_map/psum | solution.py:47
  115.3 22.9 %copy-start.4 = (f32[4,128,128]{2,1,0:T(8,128)S(1)}, f32[4,128,128]{2,1,0:T(8,128)}, u32[]{:S(2)}) copy-start(f32[4,128,128]{2,1,0:T(8,128)} %param.21) | copy-start | bytes 786436
  115.3 58.6 %copy-start.5 = (f32[2,128,128]{2,1,0:T(8,128)S(1)}, f32[2,128,128]{2,1,0:T(8,128)}, u32[]{:S(2)}) copy-start(f32[2,128,128]{2,1,0:T(8,128)} %param.20) | copy-start | bytes 393220
  115.3 84.5 %copy-start.1 = (bf16[4,4,64,1280]{3,2,1,0:T(8,128)(2,1)S(1)}, bf16[4,4,64,1280]{3,2,1,0:T(8,128)(2,1)}, u32[]{:S(2)}) copy-start(bf16[4,4,64,1280]{3,2,1,0:T(8,128)(2,1)} %param.16) | copy-start | bytes 7864324
  128.5 46.6 %copy-start.8 = (s32[4]{0:T(128)S(1)}, s32[4]{0:T(128)}, u32[]{:S(2)}) copy-start(s32[4]{0:T(128)} %param.22) | copy-start | bytes 52
  128.5 69.5 %copy-start.6 = (f32[64]{0:T(128)S(1)}, f32[64]{0:T(128)}, u32[]{:S(2)}) copy-start(f32[64]{0:T(128)} %param.23) | copy-start | bytes 772
Sparse Core Ops, SparseCore 0:
  11.4 31.3 all-reduce.8
  72.7 23.1 reduce-scatter.3
  98.1 40.0 all-reduce.6
  140.5 33.4 all-reduce.4
where the time goes:
time: 207 us; the launch traced here: 206 us
  local copies, waits for them, and re-layouts  92.7 us (45%)
  waiting for transfers between devices  47.4 us (23%)
  blocking collectives  23.8 us (11%)
  matrix products  22.5 us (11%)
  between operations  15.3 us (7%)
  other arithmetic  4.44 us (2%)
    unnamed x25, local copies, waits for them, and re-layouts  78.4 us
    psum x1, waiting for transfers between devices, per_device(): dense_full = lax.psum(dense_portion, ('expert', 'tensor'))  31.8 us
    psum x1, blocking collectives, per_device(): domain_total = lax.psum(domain_part, 'dp')  21.3 us
    reduce_scatter x1, local copies, waits for them, and re-layouts, per_device(): lax.psum_scatter(jnp.einsum('lmtd,ldr->tlmr', block, dense_proj_in, prefe...  13.2 us
    unnamed x6, waiting for transfers between devices  8.98 us
    psum x1, waiting for transfers between devices, per_device(): expert_full = lax.psum(expert_part, 'tensor')  6.66 us
    dot_general x1, matrix products, per_device(): jnp.einsum('lmtd,ldr->tlmr', dense_cot, dense_proj_out, preferred_element...  5.64 us
    dot_general x1, matrix products, per_device(): jnp.einsum('lmtd,ldr->tlmr', block, dense_proj_in, preferred_element_type...  5.62 us
  transfers between devices with their start and end apart: 4, of which 3 were waited for; matrix products, arithmetic and copies ran while one was open for 54% of the time, Pallas kernels for 0%

commit v1 on v0

--- a/solution.py
+++ b/solution.py
@@ -44,7 +44,8 @@
     expert_part = jnp.einsum(
         "cmer,cmes->mers", expert_u, expert_weight_matrix, precision=lax.Precision.HIGHEST
     )
-    dense_full = lax.psum(dense_portion, ("expert", "tensor"))
+    parts = lax.all_gather(dense_portion, ("expert", "tensor"))
+    dense_full = jnp.sum(parts, axis=0)
     dense_score = jnp.sum(dense_full * dense_valid[:, None], axis=(0, 2, 3))
     expert_full = lax.psum(expert_part, "tensor")
     expert_local = jnp.sum(expert_full * expert_valid[None], axis=(1, 2, 3))

time: 207 us -> 165 us (0.80)
  local copies, waits for them, and re-layouts: 92.7 us -> 4.46 us
  waiting for transfers between devices: 47.4 us -> 92.1 us
    unnamed x25 -> x16, local copies, waits for them, and re-layouts: 78.4 us -> 3.32 us
    psum x1, waiting for transfers between devices: 6.66 us -> 39.3 us  [per_device(): expert_full = lax.psum(expert_part, 'tensor')]
    psum x1 -> x0, waiting for transfers between devices: 31.8 us -> none  [per_device(): dense_full = lax.psum(dense_portion, ('expert', 'tensor'))]
    all_gather x0 -> x1, waiting for transfers between devices: none -> 20.1 us  [per_device(): parts = lax.all_gather(dense_portion, ('expert', 'tensor'))]
    reduce_scatter x1 -> x0, local copies, waits for them, and re-layouts: 13.2 us -> none  [per_device(): lax.psum_scatter(jnp.einsum('lmtd,ldr->tlmr', block, dense_proj_in, prefe...]
    reduce_scatter x0 -> x1, waiting for transfers between devices: none -> 12.5 us  [per_device(): lax.psum_scatter(jnp.einsum('lmtd,ldr->tlmr', block, dense_proj_in, prefe...]
    unnamed x6 -> x5, waiting for transfers between devices: 8.98 us -> 20.1 us
  transfers between devices with their start and end apart: 4 -> 4, of which waited for: 3 -> 4; matrix products, arithmetic and copies ran while one was open for 54% -> 15% of each run, Pallas kernels for 0% -> 0%
where the time goes in v1:
time: 165 us
  waiting for transfers between devices  92.1 us (56%)
  matrix products  24.1 us (15%)
  blocking collectives  23.8 us (14%)
  between operations  15.3 us (9%)
  other arithmetic  5.16 us (3%)
  local copies, waits for them, and re-layouts  4.46 us (3%)
    psum x1, waiting for transfers between devices, per_device(): expert_full = lax.psum(expert_part, 'tensor')  39.3 us
    psum x1, blocking collectives, per_device(): domain_total = lax.psum(domain_part, 'dp')  21.3 us
    all_gather x1, waiting for transfers between devices, per_device(): parts = lax.all_gather(dense_portion, ('expert', 'tensor'))  20.1 us
    unnamed x5, waiting for transfers between devices  20.1 us
    reduce_scatter x1, waiting for transfers between devices, per_device(): lax.psum_scatter(jnp.einsum('lmtd,ldr->tlmr', block, dense_proj_in, prefe...  12.5 us
    dot_general x1, matrix products, per_device(): jnp.einsum('lmtd,ldr->tlmr', block, dense_proj_in, preferred_element_type...  6.62 us
    dot_general x1, matrix products, per_device(): jnp.einsum('lmtd,ldr->tlmr', dense_cot, dense_proj_out, preferred_element...  6.22 us
    dot_general x1, matrix products, per_device(): jnp.einsum('mecd,dr->cmer', expert_cot, expert_proj_out, preferred_elemen...  3.44 us
  transfers between devices with their start and end apart: 4, of which 4 were waited for; matrix products, arithmetic and copies ran while one was open for 15% of the time, Pallas kernels for 0%

profile of v1, /device:TPU:0, one launch (start us, length us, event | category | flops | bytes accessed | tf_op | source)
XLA Modules:
  0.0 165.1 jit_solution(10873097597282123408)
XLA Ops:
  6.5 0.0 copy-start
  6.5 0.0 copy-start.1
  6.5 0.0 all-reduce.6.cloned.1.call-start
  6.5 1.7 %copy-done = bf16[4,4,64,1280]{3,2,1,0:T(8,128)(2,1)S(1)} copy-done((bf16[4,4,64,1280]{3,2,1,0:T(8,128)(2,1)S(1)}, bf16[4,4,64,1280]{3,2,1,0:T(8,128)(2,1)}, u32[]{:S(2)}) %copy-start) | copy-done | bytes 2621464
  8.3 1.8 %convolution_bitcast_fusion.1 = f32[64,4,4,128]{3,0,2,1:T(8,128)S(1)} fusion(bf16[4,4,64,1280]{3,2,1,0:T(8,128)(2,1)S(1)} %copy-done, bf16[1280,128]{1,0:T(8,128)(2,1)} %param.18), kind=kOutput, calls=%fused_computation.4 | convolution fusion | flops 335544320 | bytes 3473408 | tf_op jit(solution)/shard_map/mecf,fr->cmer/dot_general | solution.py:36
  10.1 1.1 copy.16
  11.2 0.0 all-reduce.6.cloned.1.call-update
  11.3 0.0 copy-start.6
  11.3 0.0 reduce-scatter.2.cloned.1.call-start
  11.3 0.0 copy-done.1
  11.3 6.6 %convolution_bitcast_fusion = f32[256,2,4,128]{0,3,2,1:T(8,128)} fusion(bf16[2,4,256,1792]{3,2,1,0:T(8,128)(2,1)} %param.12, bf16[2,1792,128]{2,1,0:T(8,128)(2,1)S(1)} %copy-done.1), kind=kOutput, calls=%fused_computation.2 | convolution fusion | flops 939524096 | bytes 9306112 | tf_op jit(solution)/shard_map/lmtd,ldr->tlmr/dot_general | solution.py:23
  18.0 0.0 reduce-scatter.2.cloned.1.call-update
  18.0 0.0 all-reduce.4.cloned.1.call-start
  18.0 0.0 copy-done.6
  18.0 0.6 dynamic-slice
  19.3 3.4 %fusion.6 = f32[128,4,4,32]{0,3,2,1:T(8,128)S(1)} fusion(bf16[4,4,32,3584]{3,2,1,0:T(8,128)(2,1)} %param.17, bf16[3584,128]{1,0:T(8,128)(2,1)} %param.19), kind=kOutput, calls=%fused_computation.8 | convolution fusion | flops 469762048 | bytes 4849664 | tf_op jit(solution)/shard_map/mecd,dr->cmer/dot_general | solution.py:41
  22.7 20.1 %all-reduce.6.cloned.1.call-done = f32[64,4,4,128]{3,2,1,0:T(4,128)} async-done(((f32[64,4,4,128]{3,2,1,0:T(4,128)}), f32[64,4,4,128]{3,2,1,0:T(4,128)}) %all-reduce.6.cloned.1.call-update) | async-done | bytes 524304
  42.8 1.0 constant_dynamic-slice_fusion
  43.8 2.8 %fusion.9 = f32[4,4,128,128]{3,2,1,0:T(8,128)} fusion(f32[128,4,4,32]{0,3,2,1:T(8,128)S(1)} %fusion.6, f32[32,4,4,128]{3,2,1,0:T(4,128)S(1)} %constant_dynamic-slice_fusion), kind=kOutput, calls=%fused_computation.12 | convolution fusion | flops 100663296 | bytes 1572864 | tf_op jit(solution)/shard_map/cmer,cmes->mers/dot_general | solution.py:44
  46.6 0.0 all-reduce.4.cloned.1.call-update
  46.6 0.0 copy-start.2
  46.6 0.0 all-gather.3.cloned.1.call-start
  46.6 6.2 %fusion.2 = f32[128,2,4,128]{0,3,2,1:T(8,128)S(1)} fusion(bf16[2,4,128,3584]{3,2,1,0:T(8,128)(2,1)} %param.13, bf16[2,3584,128]{2,1,0:T(8,128)(2,1)} %param.15), kind=kOutput, calls=%fused_computation.3 | convolution fusion | flops 939524096 | bytes 9699328 | tf_op jit(solution)/shard_map/lmtd,ldr->tlmr/dot_general | solution.py:28
  52.9 0.0 copy-start.3
  52.9 0.0 copy-start.5
  52.9 0.0 copy-start.4
  52.9 12.5 %reduce-scatter.2.cloned.1.call-done = f32[128,2,4,128]{0,3,2,1:T(8,128)} async-done(((f32[256,2,4,128]{0,3,2,1:T(8,128)}), f32[128,2,4,128]{0,3,2,1:T(8,128)}) %reduce-scatter.2.cloned.1.call-update) | async-done | bytes 524304 | tf_op jit(solution)/shard_map/reduce_scatter | solution.py:22
  65.4 3.0 %fusion.12 = f32[2,4,128,128]{3,2,1,0:T(8,128)} fusion(f32[128,2,4,128]{0,3,2,1:T(8,128)} %reduce-scatter.2.cloned.1.call-done, f32[128,2,4,128]{0,3,2,1:T(8,128)S(1)} %fusion.2), kind=kOutput, calls=%fused_computation.22 | convolution fusion | flops 201326592 | bytes 1572864 | tf_op jit(solution)/shard_map/fquy,fquh->quyh/dot_general | solution.py:31
  68.5 0.0 all-gather.3.cloned.1.call-update
  68.5 39.3 %all-reduce.4.cloned.1.call-done = f32[4,4,128,128]{3,2,1,0:T(8,128)} async-done(((f32[4,4,128,128]{3,2,1,0:T(8,128)}), f32[4,4,128,128]{3,2,1,0:T(8,128)}) %all-reduce.4.cloned.1.call-update) | async-done | bytes 1048592 | tf_op jit(solution)/shard_map/psum | solution.py:50
  107.9 0.0 copy-done.2
  107.9 1.4 multiply_reduce_fusion
  109.3 2.4 %psum.22 = f32[4]{0:T(128)S(1)} all-reduce(f32[4]{0:T(128)S(1)} %multiply_reduce_fusion), channel_id=1, replica_groups=mesh['dp'=8,'expert'=2,'tensor'=2] {'expert'}, use_global_device_ids=true, to_apply=%region_6.0 | all-reduce | flops 4 | bytes 32 | tf_op jit(solution)/shard_map/psum | solution.py:52
  111.7 20.1 %all-gather.3.cloned.1.call-done = f32[8,4,128,128]{3,2,1,0:T(8,128)} async-done(((f32[2,4,128,128]{3,2,1,0:T(8,128)}), f32[8,4,128,128]{3,2,1,0:T(8,128)}) %all-gather.3.cloned.1.call-update) | async-done | bytes 2097168 | tf_op jit(solution)/shard_map/all_gather | solution.py:47
  131.9 1.8 %reduce_sum.45 = f32[2,4,128,128]{3,2,1,0:T(8,128)S(1)} reduce(f32[4,2,4,128,128]{4,3,2,1,0:T(8,128)} %bitcast.42, f32[]{:T(128)} %constant.7.clone.1), dimensions={0}, to_apply=%region_1.0 | reduce | flops 393216 | bytes 2621444 | tf_op jit(solution)/shard_map/reduce_sum | solution.py:48
  133.6 0.0 copy-done.3
  133.7 0.2 multiply_reduce_fusion.1
  133.8 0.0 copy-done.5
  133.8 0.2 convolution_bitcast_fusion.2
  134.0 21.3 %psum.23 = f32[64]{0:T(128)S(1)} all-reduce(f32[64]{0:T(128)S(1)} %convolution_bitcast_fusion.2), channel_id=1, replica_groups=mesh['dp'=8,'expert'=2,'tensor'=2] {'dp'}, use_global_device_ids=true, to_apply=%region_7.0 | all-reduce | flops 64 | bytes 512 | tf_op jit(solution)/shard_map/psum | solution.py:61
  155.3 0.6 multiply_reduce_fusion.3
  156.6 0.0 copy-done.4
  156.7 0.6 multiply_reduce_fusion.2
  158.0 0.6 add_subtract_fusion
Async XLA Ops:
  6.5 1.7 %copy-start = (bf16[4,4,64,1280]{3,2,1,0:T(8,128)(2,1)S(1)}, bf16[4,4,64,1280]{3,2,1,0:T(8,128)(2,1)}, u32[]{:S(2)}) copy-start(bf16[4,4,64,1280]{3,2,1,0:T(8,128)(2,1)} %param.16) | copy-start | bytes 7864324
  6.5 4.8 %copy-start.1 = (bf16[2,1792,128]{2,1,0:T(8,128)(2,1)S(1)}, bf16[2,1792,128]{2,1,0:T(8,128)(2,1)}, u32[]{:S(2)}) copy-start(bf16[2,1792,128]{2,1,0:T(8,128)(2,1)} %param.14) | copy-start | bytes 2752516
  6.5 36.3 %all-reduce.6.cloned.1.call-start = ((), (), s32[]{:S(2)}) async-start(), calls=%async_computation.4 | async-start | bytes 1048576
  11.3 6.8 %copy-start.6 = (u32[32]{0:T(128)S(1)}, u32[32]{0:T(128)}, u32[]{:S(2)}) copy-start(u32[32]{0:T(128)} %constant.29) | copy-start | bytes 388
  11.3 54.2 %reduce-scatter.2.cloned.1.call-start = ((), (), s32[]{:S(2)}) async-start(), calls=%async_computation.1 | async-start | bytes 1572864 | tf_op jit(solution)/shard_map/reduce_scatter | solution.py:22
  18.0 89.9 %all-reduce.4.cloned.1.call-start = ((), (), s32[]{:S(2)}) async-start(), calls=%async_computation.2 | async-start | bytes 2097152 | tf_op jit(solution)/shard_map/psum | solution.py:50
  46.6 61.3 %copy-start.2 = (f32[4,128,128]{2,1,0:T(8,128)S(1)}, f32[4,128,128]{2,1,0:T(8,128)}, u32[]{:S(2)}) copy-start(f32[4,128,128]{2,1,0:T(8,128)} %param.21) | copy-start | bytes 786436
  46.6 85.3 %all-gather.3.cloned.1.call-start = ((), (), s32[]{:S(2)}) async-start(), calls=%async_computation.3 | async-start | bytes 2621440 | tf_op jit(solution)/shard_map/all_gather | solution.py:47
  52.9 80.8 %copy-start.3 = (f32[2,128,128]{2,1,0:T(8,128)S(1)}, f32[2,128,128]{2,1,0:T(8,128)}, u32[]{:S(2)}) copy-start(f32[2,128,128]{2,1,0:T(8,128)} %param.20) | copy-start | bytes 393220
  52.9 80.9 %copy-start.5 = (s32[4]{0:T(128)S(1)}, s32[4]{0:T(128)}, u32[]{:S(2)}) copy-start(s32[4]{0:T(128)} %param.22) | copy-start | bytes 52
  52.9 103.7 %copy-start.4 = (f32[64]{0:T(128)S(1)}, f32[64]{0:T(128)}, u32[]{:S(2)}) copy-start(f32[64]{0:T(128)} %param.23) | copy-start | bytes 772
Sparse Core Ops, SparseCore 0:
  11.4 31.3 all-reduce.5
  45.0 20.3 reduce-scatter.1
  67.7 40.0 all-reduce.3
  109.3 22.5 all-gather.2
